TPU v7x, 32 devices: a whole 2x2x4 slice. The times are simulated.
32 devices in a mesh: row: 4 (over x, core), col: 8 (over z, y).
Axes of the slice: x: 2, y: 2, z: 4, core: 2. Of those that a mesh axis runs over, the one named last changes fastest.
Arguments:
- matrix: float32 [2048, 8192], P('col', 'row'), may hold values from -6 to 6
- basis: float32 [8192, 512], P(('row', 'col')), may hold values from -0.0625 to 0.0625
Outputs:
- root: float32 [512, 512], P('row', 'col')
- right: float32 [2048, 512], P('col')
All inputs are finite; a program needn't handle non-finite values.
Results may differ from a plain program's by a relative error of at most 0.00018.
Values sent between devices are 32-bit elements; how exact they have to be, the bound alone decides.
A program may use at most 64 MiB of HBM per device.

v0:
```python
import jax
import jax.numpy as jnp
from jax import lax
from jax.sharding import PartitionSpec as P

ITERS = 8


def polar_steps(gram, width):
    highest = lax.Precision.HIGHEST
    scale = jnp.sqrt(jnp.sum(gram * gram) + 1e-06)
    ident = jnp.eye(width, dtype=jnp.float32)
    upper = gram / scale
    lower = ident
    for step in range(ITERS):
        middle = 0.5 * (3.0 * ident - jnp.dot(lower, upper, precision=highest))
        upper = jnp.dot(upper, middle, precision=highest)
        lower = jnp.dot(middle, lower, precision=highest)
    return (upper, lower, jnp.sqrt(scale))


def local(matrix, basis):
    highest = lax.Precision.HIGHEST
    width = basis.shape[1]
    nrow = lax.axis_size("row")
    ncol = lax.axis_size("col")
    partial_proj = lax.dot_general(
        lax.all_gather(basis, "col", axis=0, tiled=True),
        matrix,
        (((0,), (1,)), ((), ())),
        precision=highest,
    )
    proj = lax.psum(partial_proj, "row")
    gram = lax.psum(jnp.dot(proj, proj.T, precision=highest), "col")
    upper, lower, root_scale = polar_steps(gram, width)
    right = jnp.dot(proj.T, lower, precision=highest) / root_scale
    root_full = upper * root_scale
    row_len = width // nrow
    col_len = width // ncol
    root = lax.dynamic_slice(
        root_full,
        (lax.axis_index("row") * row_len, lax.axis_index("col") * col_len),
        (row_len, col_len),
    )
    return (root, right)


def solution(mesh):
    return jax.shard_map(
        local,
        mesh=mesh,
        in_specs=(P("col", "row"), P(("row", "col"), None)),
        out_specs=(P("row", "col"), P("col", None)),
        check_vma=False,
    )
```

profile of v0, /device:TPU:0, one launch (start us, length us, event | category | flops | bytes accessed | tf_op | source)
XLA Modules:
  0.0 269.0 jit_solution(109907291531495080)
XLA Ops:
  8.0 77.7 %all-gather.2.cloned.1.call-done = f32[2048,512]{1,0:T(8,128)} async-done(((f32[256,512]{1,0:T(8,128)}), f32[2048,512]{1,0:T(8,128)}) %all-gather.2.cloned.1.call-update) | async-done | bytes 4194320 | tf_op jit(solution)/shard_map/all_gather | solution.py:28
  85.7 9.6 %fusion.10 = f32[512,256]{1,0:T(8,128)} fusion(f32[2048,512]{1,0:T(8,128)} %all-gather.2.cloned.1.call-done, f32[256,2048]{1,0:T(8,128)S(1)} %copy-done), kind=kOutput, calls=%fused_computation.23 | convolution fusion | flops 3221225472 | bytes 6815744 | tf_op jit(solution)/shard_map/dot_general | solution.py:27
  95.8 31.6 %all-reduce.3.cloned.1.call-done = f32[512,256]{1,0:T(8,128)} async-done(((f32[512,256]{1,0:T(8,128)}), f32[512,256]{1,0:T(8,128)}) %all-reduce.3.cloned.1.call-update) | async-done | bytes 524304 | tf_op jit(solution)/shard_map/psum | solution.py:33
  127.4 3.2 %fusion.11 = f32[512,512]{1,0:T(8,128)} fusion(f32[512,256]{1,0:T(8,128)} %all-reduce.3.cloned.1.call-done), kind=kOutput, calls=%fused_computation.24 | convolution fusion | flops 805306368 | bytes 1572864 | tf_op jit(solution)/shard_map/dot_general | solution.py:34
  130.7 78.7 %all-reduce.5.cloned.1.call-done = f32[512,512]{1,0:T(8,128)} async-done(((f32[512,512]{1,0:T(8,128)}), f32[512,512]{1,0:T(8,128)}) %all-reduce.5.cloned.1.call-update) | async-done | bytes 1048592 | tf_op jit(solution)/shard_map/psum | solution.py:34
  209.4 2.2 multiply_reduce_fusion
  212.3 2.3 fusion.7
  215.6 1.9 fusion.9
  217.5 1.8 fusion
  219.3 1.8 fusion.12
  221.2 1.8 fusion.13
  223.0 2.0 fusion.1
  225.1 1.8 fusion.15
  228.8 1.9 fusion.2
  234.3 1.9 fusion.3
  236.2 2.1 fusion.19
  240.1 1.8 fusion.4
  242.0 1.8 fusion.21
  245.7 1.9 fusion.5
  249.4 3.1 %fusion.22 = f32[512,512]{1,0:T(8,128)} fusion(f32[512,512]{1,0:T(8,128)S(1)} %fusion.20, f32[512,512]{1,0:T(8,128)S(1)} %fusion.5), kind=kOutput, calls=%fused_computation.35 | convolution fusion | flops 1610612736 | bytes 3145728 | tf_op jit(solution)/shard_map/dot_general | solution.py:17
  252.6 3.2 %fusion.6 = f32[512,512]{1,0:T(8,128)S(1)} fusion(f32[512,512]{1,0:T(8,128)S(1)} %fusion.23, f32[512,512]{1,0:T(8,128)} %fusion.22), kind=kOutput, calls=%fused_computation.14 | convolution fusion | flops 1611661312 | bytes 3145728 | tf_op jit(solution)/shard_map/dot_general | solution.py:16
  255.8 1.8 fusion.25
  257.6 1.9 fusion.24
  260.1 1.9 convolution_divide_fusion
  (22 shorter events, 14.0 us)
Async XLA Ops:
  7.2 78.5 %copy-start = (f32[256,2048]{1,0:T(8,128)S(1)}, f32[256,2048]{1,0:T(8,128)}, u32[]{:S(2)}) copy-start(f32[256,2048]{1,0:T(8,128)} %param.2) | copy-start | bytes 6291460
  7.2 78.5 %all-gather.2.cloned.1.call-start = ((), (), s32[]{:S(2)}) async-start(), calls=%async_computation | async-start | bytes 4718592 | tf_op jit(solution)/shard_map/all_gather | solution.py:28
  7.9 119.5 %all-reduce.3.cloned.1.call-start = ((), (), s32[]{:S(2)}) async-start(), calls=%async_computation.1 | async-start | bytes 1048576 | tf_op jit(solution)/shard_map/psum | solution.py:33
  95.3 114.0 %all-reduce.5.cloned.1.call-start = ((), (), s32[]{:S(2)}) async-start(), calls=%async_computation.2 | async-start | bytes 2097152 | tf_op jit(solution)/shard_map/psum | solution.py:34
  209.4 6.2 %copy-start.3 = (f32[512,512]{1,0:T(8,128)S(1)}, f32[512,512]{1,0:T(8,128)}, u32[]{:S(2)}) copy-start(f32[512,512]{1,0:T(8,128)} %all-reduce.5.cloned.1.call-done) | copy-start | bytes 3145732
  252.6 5.1 %copy-start.1 = (f32[512,512]{1,0:T(8,128)S(1)}, f32[512,512]{1,0:T(8,128)}, u32[]{:S(2)}) copy-start(f32[512,512]{1,0:T(8,128)} %fusion.22) | copy-start | bytes 3145732
  252.6 7.6 %copy-start.2 = (f32[512,256]{1,0:T(8,128)S(1)}, f32[512,256]{1,0:T(8,128)}, u32[]{:S(2)}) copy-start(f32[512,256]{1,0:T(8,128)} %all-reduce.3.cloned.1.call-done) | copy-start | bytes 1572868
Sparse Core Ops, SparseCore 0:
  10.1 75.5 all-gather.1
  95.4 31.9 all-reduce.2
  130.9 78.3 all-reduce.4
where the time goes:
time: 274 us; the launch traced here: 269 us
  waiting for transfers between devices  189 us (69%)
  matrix products  61.7 us (23%)
  between operations  15.2 us (6%)
  other arithmetic  2.82 us (1%)
    psum x1, waiting for transfers between devices, local(): gram = lax.psum(jnp.dot(proj, proj.T, precision=highest), 'col')  78.7 us
    all_gather x1, waiting for transfers between devices, local(): lax.all_gather(basis, 'col', axis=0, tiled=True)  77.7 us
    psum x1, waiting for transfers between devices, local(): proj = lax.psum(partial_proj, 'row')  31.6 us
    dot_general x8, matrix products, polar_steps(): middle = 0.5 * (3.0 * ident - jnp.dot(lower, upper, precision=highest))  16.8 us
    dot_general x8, matrix products, polar_steps(): upper = jnp.dot(upper, middle, precision=highest)  16.1 us
    dot_general x8, matrix products, polar_steps(): lower = jnp.dot(middle, lower, precision=highest)  14.1 us
    dot_general x1, matrix products, local(): lax.dot_general(lax.all_gather(basis, 'col', axis=0, tiled=True), matrix,...  9.64 us
  transfers between devices with their start and end apart: 3, of which 3 were waited for; matrix products, arithmetic and copies ran while one was open for 0% of the time, Pallas kernels for 0%

commit v1 on v0

v1 whole, which is shorter than its diff:
```python
import functools

import jax
import jax.numpy as jnp
from jax import lax
from jax.experimental import pallas as pl
from jax.experimental.pallas import tpu as pltpu
from jax.sharding import PartitionSpec as P

ITERS = 8
OUTER = 4
MESH = pl.DeviceIdType.MESH


def split(x):
    hi = x.astype(jnp.bfloat16)
    lo = (x - hi.astype(jnp.float32)).astype(jnp.bfloat16)
    return hi, lo


def dot3(a, b, dims=(((1,), (0,)), ((), ()))):
    dot = functools.partial(lax.dot_general, dimension_numbers=dims, preferred_element_type=jnp.float32)
    return dot(a[0], b[0]) + dot(a[0], b[1]) + dot(a[1], b[0])


def kernel(
    nrow, ncol, matrix, basis, root, right,
    blocks, pieces, total, parts, plane, partial, shares, gram, power,
    basis_send, basis_recv, piece_send, piece_recv, part_send, part_recv,
    proj_send, proj_recv, share_send, share_recv, line_send, line_recv,
    gram_send, gram_recv,
):
    inner = ncol // OUTER
    nplane = nrow * inner
    row, col = lax.axis_index("row"), lax.axis_index("col")
    out, inn = col // inner, lax.rem(col, inner)
    me = row * inner + inn
    cols, depth, width = matrix.shape[0], basis.shape[0], basis.shape[1]
    high = plane.shape[0] // nplane
    tall, wide = width // nplane, width // OUTER

    def plane_peer(k):
        other = lax.rem(me + k, nplane)
        return other, {"row": other // inner, "col": out * inner + lax.rem(other, inner)}

    def line_peer(k):
        other = lax.rem(out + k, OUTER)
        return other, {"row": row, "col": other * inner + inn}

    def remote(src, dst, send, recv, device):
        return pltpu.make_async_remote_copy(
            src_ref=src, dst_ref=dst, send_sem=send, recv_sem=recv, device_id=device, device_id_type=MESH
        )

    barrier = pltpu.get_barrier_semaphore()
    for k in range(1, nplane):
        pl.semaphore_signal(barrier, inc=1, device_id=plane_peer(k)[1], device_id_type=MESH)
    for k in range(1, OUTER):
        pl.semaphore_signal(barrier, inc=1, device_id=line_peer(k)[1], device_id_type=MESH)
    pl.semaphore_wait(barrier, nplane - 1 + OUTER - 1)

    def block_copy(source, step, src):
        way = 0 if step > 0 else 1
        return remote(
            src, blocks.at[source], basis_send.at[source, way], basis_recv.at[source],
            {"row": row, "col": (out + step) * inner + inn},
        )

    def both_ways(step):
        return out < OUTER - 1 if step > 0 else out > 0

    for step in (1, -1):
        @pl.when(both_ways(step))
        def _(step=step):
            block_copy(out, step, basis).start()

    def piece_copy(k, at):
        other = lax.rem(inn + k, inner)
        device = {"row": row, "col": out * inner + other}
        start = pl.multiple_of((at * inner + other) * depth, depth)
        return remote(
            matrix.at[:, pl.ds(start, depth)], pieces.at[k - 1, at],
            piece_send.at[k - 1, at], piece_recv.at[k - 1, at], device,
        )

    for d in range(OUTER):
        for k in range(1, inner):
            piece_copy(k, lax.rem(out + d, OUTER)).start()

    def add_block(at, block, first=False):
        halves = split(block[...])
        for k in range(inner):
            if k == 0:
                start = pl.multiple_of((at * inner + inn) * depth, depth)
                mine = matrix[:, pl.ds(start, depth)]
            else:
                piece_copy(k, at).wait_recv()
                mine = pieces[k - 1, at]
            home = pl.ds(pl.multiple_of(lax.rem(inn + inner - k, inner) * cols, cols), cols)
            got = dot3(split(mine), halves)
            total[home, :] = got if first else total[home, :] + got

    add_block(out, basis, True)
    for d in range(1, OUTER):
        for step in (1, -1):
            source = out - step * d

            @pl.when((source >= 0) & (source < OUTER))
            def _(source=source, step=step):
                block_copy(source, step, blocks.at[source]).wait_recv()

                @pl.when(both_ways(step))
                def _():
                    block_copy(source, step, blocks.at[source]).start()

        for step in (1, -1):
            source = out - step * d

            @pl.when((source >= 0) & (source < OUTER))
            def _(source=source, step=step):
                add_block(source, blocks.at[source])

    copies = []
    for k in range(1, nplane):
        other, device = plane_peer(k)
        copy = remote(
            total.at[pl.ds(pl.multiple_of(other * high, high), high), :], parts.at[k - 1],
            part_send.at[k - 1], part_recv.at[k - 1], device,
        )
        copy.start()
        copies.append(copy)
    own = pl.ds(pl.multiple_of(me * high, high), high)
    mine = total[own, :]
    for k, copy in enumerate(copies):
        copy.wait_recv()
        mine = mine + parts[k]
    plane[own, :] = mine

    def proj_copy(k, at):
        spot = plane.at[pl.ds(pl.multiple_of(at * high, high), high), :]
        return remote(spot, spot, proj_send.at[k - 1], proj_recv.at[k - 1], plane_peer(k)[1])

    for k in range(1, nplane):
        proj_copy(k, me).start()
    for k in range(1, nplane):
        proj_copy(k, lax.rem(me + nplane - k, nplane)).wait_recv()

    proj = split(plane[...])
    partial[...] = dot3(proj, proj, (((0,), (0,)), ((), ())))

    band = pl.ds(pl.multiple_of(me * tall, tall), tall)

    def lanes(at):
        return pl.ds(pl.multiple_of(at * wide, wide), wide)

    shared = []
    for k in range(1, OUTER):
        other, device = line_peer(k)
        copy = remote(
            partial.at[band, lanes(other)], shares.at[k - 1],
            share_send.at[k - 1], share_recv.at[k - 1], device,
        )
        copy.start()
        shared.append(copy)
    mine = partial[band, lanes(out)]
    for k, copy in enumerate(shared):
        copy.wait_recv()
        mine = mine + shares[k]
    gram[band, lanes(out)] = mine

    def line_copy(k, at):
        spot = gram.at[band, lanes(at)]
        return remote(spot, spot, line_send.at[k - 1], line_recv.at[k - 1], line_peer(k)[1])

    for k in range(1, OUTER):
        line_copy(k, out).start()
    for k in range(1, OUTER):
        line_copy(k, lax.rem(out + OUTER - k, OUTER)).wait_recv()

    def gram_copy(k, at):
        spot = gram.at[pl.ds(pl.multiple_of(at * tall, tall), tall), :]
        return remote(spot, spot, gram_send.at[k - 1], gram_recv.at[k - 1], plane_peer(k)[1])

    for k in range(1, nplane):
        gram_copy(k, me).start()
    for k in range(1, nplane):
        gram_copy(k, lax.rem(me + nplane - k, nplane)).wait_recv()

    whole = gram[...]
    scale = jnp.sqrt(jnp.sum(whole * whole, keepdims=True) + 1e-06)
    ident = (
        lax.broadcasted_iota(jnp.int32, (width, width), 0) == lax.broadcasted_iota(jnp.int32, (width, width), 1)
    ).astype(jnp.float32)
    power[...] = whole / scale
    root_scale = jnp.sqrt(scale)
    rows = root.shape[0]
    root[...] = gram[pl.ds(pl.multiple_of(row * rows, rows), rows), :] / scale
    right[...] = plane[pl.ds(pl.multiple_of(inn * cols, cols), cols), :]

    def polar(step, carry):
        now = power[...]
        middle = split(1.5 * ident - 0.5 * now)
        root[...] = dot3(split(root[...]), middle)
        right[...] = dot3(split(right[...]), middle)
        half = dot3(split(now), middle)
        power[...] = dot3(split(half), middle)
        return carry

    lax.fori_loop(0, ITERS - 1, polar, 0)
    middle = split(1.5 * ident - 0.5 * power[...])
    root[...] = dot3(split(root[...]), middle) * root_scale
    right[...] = dot3(split(right[...]), middle) / root_scale

    for step in (1, -1):
        @pl.when(both_ways(step))
        def _(step=step):
            block_copy(out, step, basis).wait_send()
    for d in range(1, OUTER):
        for step in (1, -1):
            source = out - step * d

            @pl.when((source >= 0) & (source < OUTER) & both_ways(step))
            def _(source=source, step=step):
                block_copy(source, step, blocks.at[source]).wait_send()
    for d in range(OUTER):
        for k in range(1, inner):
            piece_copy(k, lax.rem(out + d, OUTER)).wait_send()
    for copy in copies + shared:
        copy.wait_send()
    for k in range(1, nplane):
        proj_copy(k, me).wait_send()
        gram_copy(k, me).wait_send()
    for k in range(1, OUTER):
        line_copy(k, out).wait_send()


def solution(mesh):
    nrow, ncol = mesh.shape["row"], mesh.shape["col"]
    inner = ncol // OUTER
    nplane = nrow * inner

    def local(matrix, basis):
        cols, (depth, width) = matrix.shape[0], basis.shape
        tall = inner * cols
        dma = pltpu.SemaphoreType.DMA
        vmem = pl.BlockSpec(memory_space=pltpu.VMEM)
        root_rows, right = pl.pallas_call(
            functools.partial(kernel, nrow, ncol),
            out_shape=(
                jax.ShapeDtypeStruct((width // nrow, width), jnp.float32),
                jax.ShapeDtypeStruct((cols, width), jnp.float32),
            ),
            in_specs=[vmem, vmem],
            out_specs=(vmem, vmem),
            scratch_shapes=[
                pltpu.VMEM((OUTER, depth, width), jnp.float32),
                pltpu.VMEM((inner - 1, OUTER, cols, depth), jnp.float32),
                pltpu.VMEM((tall, width), jnp.float32),
                pltpu.VMEM((nplane - 1, tall // nplane, width), jnp.float32),
                pltpu.VMEM((tall, width), jnp.float32),
                pltpu.VMEM((width, width), jnp.float32),
                pltpu.VMEM((OUTER - 1, width // nplane, width // OUTER), jnp.float32),
                pltpu.VMEM((width, width), jnp.float32),
                pltpu.VMEM((width, width), jnp.float32),
                dma((OUTER, 2)),
                dma((OUTER,)),
                dma((inner - 1, OUTER)),
                dma((inner - 1, OUTER)),
                dma((nplane - 1,)),
                dma((nplane - 1,)),
                dma((nplane - 1,)),
                dma((nplane - 1,)),
                dma((OUTER - 1,)),
                dma((OUTER - 1,)),
                dma((OUTER - 1,)),
                dma((OUTER - 1,)),
                dma((nplane - 1,)),
                dma((nplane - 1,)),
            ],
            compiler_params=pltpu.CompilerParams(
                collective_id=0, has_side_effects=True, vmem_limit_bytes=56 * 1024 * 1024
            ),
        )(matrix, basis)
        start = lax.axis_index("col") * (width // ncol)
        return lax.dynamic_slice(root_rows, (0, start), (width // nrow, width // ncol)), right

    return jax.shard_map(
        local,
        mesh=mesh,
        in_specs=(P("col", "row"), P(("row", "col"), None)),
        out_specs=(P("row", "col"), P("col", None)),
        check_vma=False,
    )
```

time: 274 us -> 115 us (0.42)
  the two profiles are of different devices: /device:TPU:0 before, /device:TPU:1 now
where the time goes in v1:
time: 115 us; the launch traced here: 114 us
  Pallas kernels  110 us (96%)
  local copies, waits for them, and re-layouts  3.5 us (3%)
    pallas_call x1, Pallas kernels, local(): pl.pallas_call(functools.partial(kernel, nrow, ncol), out_shape=(jax.Shap...  110 us
    unnamed x2, local copies, waits for them, and re-layouts  2.57 us

profile of v1, /device:TPU:1, one launch (start us, length us, event | category | flops | bytes accessed | tf_op | source)
XLA Modules:
  0.0 114.4 jit_solution(7582890581676368549)
XLA Ops:
  0.6 110.3 %shard_map.41 = (f32[128,512]{1,0:T(8,128)}, f32[256,512]{1,0:T(8,128)}) custom-call(f32[256,2048]{1,0:T(8,128)} %matrix.1, f32[256,512]{1,0:T(8,128)} %basis.1), custom_call_target="tpu_custom_call" | custom-call | tf_op jit(solution)/shard_map/pallas_call | solution.py:247
  110.9 0.9 constant_dynamic-slice_fusion
  111.8 0.7 copy.4
  112.5 1.9 %copy.6 = f32[256,512]{1,0:T(8,128)} copy(f32[256,512]{1,0:T(8,128)} %get-tuple-element.11) | data formatting | bytes 1048576

commit v2 on v1

v2 whole, which is shorter than its diff:
```python
import functools

import jax
import jax.numpy as jnp
from jax import lax
from jax.experimental import pallas as pl
from jax.experimental.pallas import tpu as pltpu
from jax.sharding import PartitionSpec as P

ITERS = 8
OUTER = 4
CHUNKS = 2
MESH = pl.DeviceIdType.MESH


def split(x):
    hi = x.astype(jnp.bfloat16)
    lo = (x - hi.astype(jnp.float32)).astype(jnp.bfloat16)
    return hi, lo


def dot3(a, b, dims=(((1,), (0,)), ((), ()))):
    dot = functools.partial(lax.dot_general, dimension_numbers=dims, preferred_element_type=jnp.float32)
    return dot(a[0], b[0]) + dot(a[0], b[1]) + dot(a[1], b[0])


def kernel(
    nrow, ncol, matrix, basis, root, right, norm,
    blocks, pieces, total, halves, parts, plane, partial, shares, gram, work,
    basis_send, basis_recv, piece_send, piece_recv, half_send, half_recv, part_send, part_recv,
    share_send, share_recv, line_send, line_recv,
    proj_send, proj_recv, mate_send, mate_recv,
    gram_send, gram_recv, twin_send, twin_recv,
):
    inner = ncol // OUTER
    nchip = nrow // 2 * inner
    row, col = lax.axis_index("row"), lax.axis_index("col")
    out, inn = col // inner, lax.rem(col, inner)
    core = lax.rem(row, 2)
    chip = row // 2 * inner + inn
    me = core * nchip + chip
    cols, depth, width = matrix.shape[0], basis.shape[0], basis.shape[1]
    high = plane.shape[0] // (2 * nchip)
    tall, wide = width // (2 * nchip), width // OUTER
    piece = depth // CHUNKS
    mate = {"row": row + 1 - 2 * core, "col": col}

    def chip_at(k):
        return lax.rem(chip + k, nchip)

    def chip_peer(k):
        other = chip_at(k)
        return {"row": other // inner * 2 + core, "col": out * inner + lax.rem(other, inner)}

    def line_peer(k):
        other = lax.rem(out + k, OUTER)
        return other, {"row": row, "col": other * inner + inn}

    def remote(src, dst, send, recv, device):
        return pltpu.make_async_remote_copy(
            src_ref=src, dst_ref=dst, send_sem=send, recv_sem=recv, device_id=device, device_id_type=MESH
        )

    barrier = pltpu.get_barrier_semaphore()
    greeted = [mate] + [chip_peer(k) for k in range(1, nchip)] + [line_peer(k)[1] for k in range(1, OUTER)]
    for device in greeted:
        pl.semaphore_signal(barrier, inc=1, device_id=device, device_id_type=MESH)
    pl.semaphore_wait(barrier, len(greeted))

    def block_copy(source, step, chunk, own=False):
        way = 0 if step > 0 else 1
        lines = pl.ds(chunk * piece, piece)
        here = blocks.at[source, lines, :]
        return remote(
            basis.at[lines, :] if own else here, here,
            basis_send.at[source, way, chunk], basis_recv.at[source, chunk],
            {"row": row, "col": (out + step) * inner + inn},
        )

    def both_ways(step):
        return out < OUTER - 1 if step > 0 else out > 0

    for step in (1, -1):
        @pl.when(both_ways(step))
        def _(step=step):
            for chunk in range(CHUNKS):
                block_copy(out, step, chunk, True).start()

    def piece_copy(k, at):
        other = lax.rem(inn + k, inner)
        device = {"row": row, "col": out * inner + other}
        start = pl.multiple_of((at * inner + other) * depth, depth)
        return remote(
            matrix.at[:, pl.ds(start, depth)], pieces.at[k - 1, at],
            piece_send.at[k - 1, at], piece_recv.at[k - 1, at], device,
        )

    for d in range(OUTER):
        for k in range(1, inner):
            piece_copy(k, lax.rem(out + d, OUTER)).start()

    def add_block(at, block, first=False):
        block_halves = split(block[...])
        for k in range(inner):
            if k == 0:
                start = pl.multiple_of((at * inner + inn) * depth, depth)
                mine = matrix[:, pl.ds(start, depth)]
            else:
                piece_copy(k, at).wait_recv()
                mine = pieces[k - 1, at]
            home = pl.ds(pl.multiple_of(lax.rem(inn + inner - k, inner) * cols, cols), cols)
            got = dot3(split(mine), block_halves)
            total[home, :] = got if first else total[home, :] + got

    add_block(out, basis, True)
    for d in range(1, OUTER):
        for chunk in range(CHUNKS):
            for step in (1, -1):
                source = out - step * d

                @pl.when((source >= 0) & (source < OUTER))
                def _(source=source, step=step, chunk=chunk):
                    block_copy(source, step, chunk).wait_recv()

                    @pl.when(both_ways(step))
                    def _():
                        block_copy(source, step, chunk).start()

        for step in (1, -1):
            source = out - step * d

            @pl.when((source >= 0) & (source < OUTER))
            def _(source=source, step=step):
                add_block(source, blocks.at[source])

    def part(which, at):
        return pl.ds(pl.multiple_of((which * nchip + at) * high, high), high)

    order = list(range(1, nchip)) + [0]

    def half_copy(k):
        return remote(
            total.at[part(1 - core, chip_at(k)), :], halves.at[k], half_send.at[k], half_recv.at[k], mate
        )

    def part_copy(k):
        return remote(
            total.at[part(core, chip_at(k)), :], parts.at[k - 1], part_send.at[k - 1], part_recv.at[k - 1], chip_peer(k)
        )

    for k in order:
        half_copy(k).start()
    for at, k in enumerate(order):
        half_copy(k).wait_recv()
        spot = part(core, chip_at(k))
        total[spot, :] = total[spot, :] + halves[k]
        if at:
            part_copy(order[at - 1]).start()
    mine = total[part(core, chip), :]
    for k in range(1, nchip):
        part_copy(k).wait_recv()
        mine = mine + parts[k - 1]
    plane[part(core, chip), :] = mine

    def gather(buffer, size, send, recv, pair_send, pair_recv):
        def copy(which, at, send_sem, recv_sem, device):
            spot = buffer.at[pl.ds(pl.multiple_of((which * nchip + at) * size, size), size), :]
            return remote(spot, spot, send_sem, recv_sem, device)

        def from_chip(k):
            return lax.rem(chip + nchip - k, nchip)

        def away(k, at):
            return copy(core, at, send.at[k - 1], recv.at[k - 1], chip_peer(k))

        def across(k, which):
            return copy(which, from_chip(k), pair_send.at[k], pair_recv.at[k], mate)

        for k in range(1, nchip):
            away(k, chip).start()
        across(0, core).start()
        for k in range(1, nchip):
            away(k, from_chip(k)).wait_recv()
            across(k, core).start()
        for k in range(nchip):
            across(k, 1 - core).wait_recv()

        def finish():
            for k in range(1, nchip):
                away(k, chip).wait_send()
            for k in range(nchip):
                across(k, core).wait_send()

        return finish

    finish_proj = gather(plane, high, proj_send, proj_recv, mate_send, mate_recv)

    proj = split(plane[...])
    partial[...] = dot3(proj, proj, (((0,), (0,)), ((), ())))

    band = pl.ds(pl.multiple_of(me * tall, tall), tall)

    def lanes(at):
        return pl.ds(pl.multiple_of(at * wide, wide), wide)

    shared = []
    for k in range(1, OUTER):
        other, device = line_peer(k)
        copy = remote(
            partial.at[band, lanes(other)], shares.at[k - 1],
            share_send.at[k - 1], share_recv.at[k - 1], device,
        )
        copy.start()
        shared.append(copy)
    mine = partial[band, lanes(out)]
    for k, copy in enumerate(shared):
        copy.wait_recv()
        mine = mine + shares[k]
    gram[band, lanes(out)] = mine

    def line_copy(k, at):
        spot = gram.at[band, lanes(at)]
        return remote(spot, spot, line_send.at[k - 1], line_recv.at[k - 1], line_peer(k)[1])

    for k in range(1, OUTER):
        line_copy(k, out).start()
    for k in range(1, OUTER):
        line_copy(k, lax.rem(out + OUTER - k, OUTER)).wait_recv()

    finish_gram = gather(gram, tall, gram_send, gram_recv, twin_send, twin_recv)

    whole = gram[...]
    scale = jnp.sqrt(jnp.sum(whole * whole, keepdims=True) + 1e-06)
    ident = (
        lax.broadcasted_iota(jnp.int32, (width, width), 0) == lax.broadcasted_iota(jnp.int32, (width, width), 1)
    ).astype(jnp.float32)
    norm[...] = jnp.broadcast_to(jnp.sqrt(scale), norm.shape)
    rows = root.shape[0]
    work[0:width, :] = whole / scale
    work[width : width + cols, :] = plane[pl.ds(pl.multiple_of(inn * cols, cols), cols), :]
    work[width + cols :, :] = gram[pl.ds(pl.multiple_of(col * rows, rows), rows), :] / scale

    def polar(step, carry):
        middle = split(1.5 * ident - 0.5 * work[0:width, :])
        got = dot3(split(work[...]), middle)
        work[width:, :] = got[width:, :]
        work[0:width, :] = dot3(split(got[:width, :]), middle)
        return carry

    lax.fori_loop(0, ITERS - 1, polar, 0)
    middle = split(1.5 * ident - 0.5 * work[0:width, :])
    got = dot3(split(work[width:, :]), middle)
    right[...] = got[:cols, :]
    root[...] = got[cols:, :]

    for step in (1, -1):
        @pl.when(both_ways(step))
        def _(step=step):
            for chunk in range(CHUNKS):
                block_copy(out, step, chunk, True).wait_send()
    for d in range(1, OUTER):
        for step in (1, -1):
            source = out - step * d

            @pl.when((source >= 0) & (source < OUTER) & both_ways(step))
            def _(source=source, step=step):
                for chunk in range(CHUNKS):
                    block_copy(source, step, chunk).wait_send()
    for d in range(OUTER):
        for k in range(1, inner):
            piece_copy(k, lax.rem(out + d, OUTER)).wait_send()
    for k in range(nchip):
        half_copy(k).wait_send()
    for k in range(1, nchip):
        part_copy(k).wait_send()
    for copy in shared:
        copy.wait_send()
    for k in range(1, OUTER):
        line_copy(k, out).wait_send()
    finish_proj()
    finish_gram()


def solution(mesh):
    nrow, ncol = mesh.shape["row"], mesh.shape["col"]
    inner = ncol // OUTER
    nchip = nrow // 2 * inner

    def local(matrix, basis):
        cols, (depth, width) = matrix.shape[0], basis.shape
        tall = inner * cols
        vmem = pl.BlockSpec(memory_space=pltpu.VMEM)

        def array(*shape):
            return pltpu.VMEM(shape, jnp.float32)

        def pair(*shape):
            return [pltpu.SemaphoreType.DMA(shape)] * 2

        root, right, norm = pl.pallas_call(
            functools.partial(kernel, nrow, ncol),
            out_shape=(
                jax.ShapeDtypeStruct((width // ncol, width), jnp.float32),
                jax.ShapeDtypeStruct((cols, width), jnp.float32),
                jax.ShapeDtypeStruct((8, 128), jnp.float32),
            ),
            in_specs=[vmem, vmem],
            out_specs=(vmem, vmem, vmem),
            scratch_shapes=[
                array(OUTER, depth, width),
                array(inner - 1, OUTER, cols, depth),
                array(tall, width),
                array(nchip, tall // (2 * nchip), width),
                array(nchip - 1, tall // (2 * nchip), width),
                array(tall, width),
                array(width, width),
                array(OUTER - 1, width // (2 * nchip), width // OUTER),
                array(width, width),
                array(width + cols + width // ncol, width),
                pltpu.SemaphoreType.DMA((OUTER, 2, CHUNKS)),
                pltpu.SemaphoreType.DMA((OUTER, CHUNKS)),
                *pair(inner - 1, OUTER),
                *pair(nchip),
                *pair(nchip - 1),
                *pair(OUTER - 1),
                *pair(OUTER - 1),
                *pair(nchip - 1),
                *pair(nchip),
                *pair(nchip - 1),
                *pair(nchip),
            ],
            compiler_params=pltpu.CompilerParams(
                collective_id=0, has_side_effects=True, vmem_limit_bytes=40 * 1024 * 1024
            ),
        )(matrix, basis)
        root_scale = norm[0, 0]
        long = width // nrow
        part = lax.dynamic_slice(root, (0, lax.axis_index("row") * long), (width // ncol, long))
        return part.T * root_scale, right / root_scale

    return jax.shard_map(
        local,
        mesh=mesh,
        in_specs=(P("col", "row"), P(("row", "col"), None)),
        out_specs=(P("row", "col"), P("col", None)),
        check_vma=False,
    )
```

time: 115 us -> 103 us (0.90)
  Pallas kernels: 110 us -> 96.2 us
  other arithmetic: 0 us -> 2.74 us
    pallas_call x1, Pallas kernels: 110 us -> 96.2 us  [local(): pl.pallas_call(functools.partial(kernel, nrow, ncol), out_shape=(jax.Shap...]
    div x0 -> x1, other arithmetic: none -> 1.49 us  [local(): return (part.T * root_scale, right / root_scale)]
    mul x0 -> x1, other arithmetic: none -> 1.26 us  [local(): return (part.T * root_scale, right / root_scale)]
    unnamed x2 -> x4, local copies, waits for them, and re-layouts: 2.57 us -> 2.63 us
where the time goes in v2:
time: 103 us
  Pallas kernels  96.2 us (93%)
  local copies, waits for them, and re-layouts  3.2 us (3%)
  other arithmetic  2.74 us (3%)
    pallas_call x1, Pallas kernels, local(): pl.pallas_call(functools.partial(kernel, nrow, ncol), out_shape=(jax.Shap...  96.2 us
    unnamed x4, local copies, waits for them, and re-layouts  2.63 us

profile of v2, /device:TPU:1, one launch (start us, length us, event | category | flops | bytes accessed | tf_op | source)
XLA Modules:
  0.0 102.8 jit_solution(11890951427652996972)
XLA Ops:
  0.6 0.0 copy-start
  0.6 1.6 %copy-done = f32[256,2048]{1,0:T(8,128)S(1)} copy-done((f32[256,2048]{1,0:T(8,128)S(1)}, f32[256,2048]{1,0:T(8,128)}, u32[]{:S(2)}) %copy-start) | copy-done | bytes 2097176
  2.2 0.0 copy-start.1
  2.2 1.0 %copy-done.1 = f32[256,512]{1,0:T(8,128)S(1)} copy-done((f32[256,512]{1,0:T(8,128)S(1)}, f32[256,512]{1,0:T(8,128)}, u32[]{:S(2)}) %copy-start.1) | copy-done | bytes 524312
  3.3 96.2 %shard_map.41 = (f32[64,512]{1,0:T(8,128)S(1)}, f32[256,512]{1,0:T(8,128)S(1)}, f32[8,128]{1,0:T(8,128)S(1)}) custom-call(f32[256,2048]{1,0:T(8,128)S(1)} %copy-done, f32[256,512]{1,0:T(8,128)S(1)} %copy-done.1), custom_call_target="tpu_custom_call" | custom-call | tf_op jit(solution)/shard_map/pallas_call | solution.py:300
  99.4 0.6 slice.3
  100.0 1.3 %multiply_bitcast_fusion = f32[128,64]{0,1:T(8,128)} fusion(f32[64,512]{1,0:T(8,128)S(1)} %get-tuple-element.5, s32[]{:T(128)S(6)} %select_n.3, f32[]{:T(128)} %bitcast), kind=kLoop, calls=%fused_computation.1 | loop fusion | flops 8192 | bytes 65544 | tf_op jit(solution)/shard_map/mul | solution.py:339
  101.3 1.5 %broadcast_divide_fusion = f32[256,512]{1,0:T(8,128)} fusion(f32[256,512]{1,0:T(8,128)S(1)} %get-tuple-element.7, f32[]{:T(128)} %bitcast), kind=kLoop, calls=%fused_computation | loop fusion | flops 131072 | bytes 1048580 | tf_op jit(solution)/shard_map/div | solution.py:339
Async XLA Ops:
  0.6 1.6 %copy-start = (f32[256,2048]{1,0:T(8,128)S(1)}, f32[256,2048]{1,0:T(8,128)}, u32[]{:S(2)}) copy-start(f32[256,2048]{1,0:T(8,128)} %matrix.1) | copy-start | bytes 6291460
  2.2 1.0 %copy-start.1 = (f32[256,512]{1,0:T(8,128)S(1)}, f32[256,512]{1,0:T(8,128)}, u32[]{:S(2)}) copy-start(f32[256,512]{1,0:T(8,128)} %basis.1) | copy-start | bytes 1572868

commit v3 on v2

--- a/solution.py
+++ b/solution.py
@@ -10,6 +10,7 @@
 ITERS = 8
 OUTER = 4
 CHUNKS = 2
+LANES = 128
 MESH = pl.DeviceIdType.MESH
 
 
@@ -25,12 +26,12 @@
 
 
 def kernel(
-    nrow, ncol, matrix, basis, root, right, norm,
-    blocks, pieces, total, halves, parts, plane, partial, shares, gram, work,
+    nrow, ncol, matrix, basis, root, right,
+    slab, base, blocks, pieces, total, halves, parts, plane, partial, shares, gram, work,
     basis_send, basis_recv, piece_send, piece_recv, half_send, half_recv, part_send, part_recv,
     share_send, share_recv, line_send, line_recv,
     proj_send, proj_recv, mate_send, mate_recv,
-    gram_send, gram_recv, twin_send, twin_recv,
+    gram_send, gram_recv, twin_send, twin_recv, load,
 ):
     inner = ncol // OUTER
     nchip = nrow // 2 * inner
@@ -61,6 +62,9 @@
             src_ref=src, dst_ref=dst, send_sem=send, recv_sem=recv, device_id=device, device_id_type=MESH
         )
 
+    loads = [pltpu.make_async_copy(basis, base, load.at[0]), pltpu.make_async_copy(matrix, slab, load.at[1])]
+    for copy in loads:
+        copy.start()
     barrier = pltpu.get_barrier_semaphore()
     greeted = [mate] + [chip_peer(k) for k in range(1, nchip)] + [line_peer(k)[1] for k in range(1, OUTER)]
     for device in greeted:
@@ -104,7 +108,7 @@
         for k in range(inner):
             if k == 0:
                 start = pl.multiple_of((at * inner + inn) * depth, depth)
-                mine = matrix[:, pl.ds(start, depth)]
+                mine = slab[:, pl.ds(start, depth)]
             else:
                 piece_copy(k, at).wait_recv()
                 mine = pieces[k - 1, at]
@@ -112,7 +116,9 @@
             got = dot3(split(mine), block_halves)
             total[home, :] = got if first else total[home, :] + got
 
-    add_block(out, basis, True)
+    for copy in loads:
+        copy.wait()
+    add_block(out, base, True)
     for d in range(1, OUTER):
         for chunk in range(CHUNKS):
             for step in (1, -1):
@@ -196,9 +202,12 @@
     finish_proj = gather(plane, high, proj_send, proj_recv, mate_send, mate_recv)
 
     proj = split(plane[...])
-    partial[...] = dot3(proj, proj, (((0,), (0,)), ((), ())))
+    around = me * tall // LANES * LANES
+    some = split(plane[:, pl.ds(pl.multiple_of(around, LANES), LANES)])
+    partial[...] = dot3(some, proj, (((0,), (0,)), ((), ())))
 
     band = pl.ds(pl.multiple_of(me * tall, tall), tall)
+    inside = pl.ds(pl.multiple_of(me * tall - around, tall), tall)
 
     def lanes(at):
         return pl.ds(pl.multiple_of(at * wide, wide), wide)
@@ -207,12 +216,12 @@
     for k in range(1, OUTER):
         other, device = line_peer(k)
         copy = remote(
-            partial.at[band, lanes(other)], shares.at[k - 1],
+            partial.at[inside, lanes(other)], shares.at[k - 1],
             share_send.at[k - 1], share_recv.at[k - 1], device,
         )
         copy.start()
         shared.append(copy)
-    mine = partial[band, lanes(out)]
+    mine = partial[inside, lanes(out)]
     for k, copy in enumerate(shared):
         copy.wait_recv()
         mine = mine + shares[k]
@@ -234,7 +243,7 @@
     ident = (
         lax.broadcasted_iota(jnp.int32, (width, width), 0) == lax.broadcasted_iota(jnp.int32, (width, width), 1)
     ).astype(jnp.float32)
-    norm[...] = jnp.broadcast_to(jnp.sqrt(scale), norm.shape)
+    root_scale = jnp.sqrt(scale)
     rows = root.shape[0]
     work[0:width, :] = whole / scale
     work[width : width + cols, :] = plane[pl.ds(pl.multiple_of(inn * cols, cols), cols), :]
@@ -250,8 +259,8 @@
     lax.fori_loop(0, ITERS - 1, polar, 0)
     middle = split(1.5 * ident - 0.5 * work[0:width, :])
     got = dot3(split(work[width:, :]), middle)
-    right[...] = got[:cols, :]
-    root[...] = got[cols:, :]
+    right[...] = got[:cols, :] / root_scale
+    root[...] = got[cols:, :] * root_scale
 
     for step in (1, -1):
         @pl.when(both_ways(step))
@@ -297,23 +306,24 @@
         def pair(*shape):
             return [pltpu.SemaphoreType.DMA(shape)] * 2
 
-        root, right, norm = pl.pallas_call(
+        root, right = pl.pallas_call(
             functools.partial(kernel, nrow, ncol),
             out_shape=(
                 jax.ShapeDtypeStruct((width // ncol, width), jnp.float32),
                 jax.ShapeDtypeStruct((cols, width), jnp.float32),
-                jax.ShapeDtypeStruct((8, 128), jnp.float32),
             ),
-            in_specs=[vmem, vmem],
-            out_specs=(vmem, vmem, vmem),
+            in_specs=[pl.BlockSpec(memory_space=pltpu.HBM)] * 2,
+            out_specs=(vmem, vmem),
             scratch_shapes=[
+                array(*matrix.shape),
+                array(depth, width),
                 array(OUTER, depth, width),
                 array(inner - 1, OUTER, cols, depth),
                 array(tall, width),
                 array(nchip, tall // (2 * nchip), width),
                 array(nchip - 1, tall // (2 * nchip), width),
                 array(tall, width),
-                array(width, width),
+                array(LANES, width),
                 array(OUTER - 1, width // (2 * nchip), width // OUTER),
                 array(width, width),
                 array(width + cols + width // ncol, width),
@@ -328,15 +338,15 @@
                 *pair(nchip),
                 *pair(nchip - 1),
                 *pair(nchip),
+                pltpu.SemaphoreType.DMA((2,)),
             ],
             compiler_params=pltpu.CompilerParams(
                 collective_id=0, has_side_effects=True, vmem_limit_bytes=40 * 1024 * 1024
             ),
         )(matrix, basis)
-        root_scale = norm[0, 0]
         long = width // nrow
         part = lax.dynamic_slice(root, (0, lax.axis_index("row") * long), (width // ncol, long))
-        return part.T * root_scale, right / root_scale
+        return part.T, right
 
     return jax.shard_map(
         local,

time: 103 us -> 101 us (0.981)
  other arithmetic: 2.74 us -> 0 us
    div x1 -> x0, other arithmetic: 1.49 us -> none  [local(): return (part.T * root_scale, right / root_scale)]
    mul x1 -> x0, other arithmetic: 1.26 us -> none  [local(): return (part.T * root_scale, right / root_scale)]
    unnamed x4 -> x5, local copies, waits for them, and re-layouts: 2.63 us -> 3.42 us
where the time goes in v3:
time: 101 us
  Pallas kernels  96.1 us (95%)
  local copies, waits for them, and re-layouts  4.05 us (4%)
    pallas_call x1, Pallas kernels, local(): pl.pallas_call(functools.partial(kernel, nrow, ncol), out_shape=(jax.Shap...  96.1 us
    unnamed x5, local copies, waits for them, and re-layouts  3.42 us

profile of v3, /device:TPU:1, one launch (start us, length us, event | category | flops | bytes accessed | tf_op | source)
XLA Modules:
  0.0 100.8 jit_solution(8902371576047399403)
XLA Ops:
  0.6 0.0 copy-start
  0.6 1.6 %copy-done = f32[256,2048]{1,0:T(8,128)S(1)} copy-done((f32[256,2048]{1,0:T(8,128)S(1)}, f32[256,2048]{1,0:T(8,128)}, u32[]{:S(2)}) %copy-start) | copy-done | bytes 2097176
  2.2 0.0 copy-start.1
  2.2 1.0 %copy-done.1 = f32[256,512]{1,0:T(8,128)S(1)} copy-done((f32[256,512]{1,0:T(8,128)S(1)}, f32[256,512]{1,0:T(8,128)}, u32[]{:S(2)}) %copy-start.1) | copy-done | bytes 524312
  3.3 96.1 %shard_map.41 = (f32[64,512]{1,0:T(8,128)S(1)}, f32[256,512]{1,0:T(8,128)S(1)}) custom-call(f32[256,2048]{1,0:T(8,128)S(1)} %copy-done, f32[256,512]{1,0:T(8,128)S(1)} %copy-done.1), custom_call_target="tpu_custom_call" | custom-call | tf_op jit(solution)/shard_map/pallas_call | solution.py:309
  99.3 0.6 dynamic-slice_bitcast_fusion
  100.0 0.8 copy.5
Async XLA Ops:
  0.6 1.6 %copy-start = (f32[256,2048]{1,0:T(8,128)S(1)}, f32[256,2048]{1,0:T(8,128)}, u32[]{:S(2)}) copy-start(f32[256,2048]{1,0:T(8,128)} %matrix.1) | copy-start | bytes 6291460
  2.2 1.0 %copy-start.1 = (f32[256,512]{1,0:T(8,128)S(1)}, f32[256,512]{1,0:T(8,128)}, u32[]{:S(2)}) copy-start(f32[256,512]{1,0:T(8,128)} %basis.1) | copy-start | bytes 1572868
